TPU v7x, 512 devices: a 8x2x16 block of a 8x8x16 slice. The times are simulated.
512 devices in a mesh: subj: 2 (over y), row: 16 (over x, core), col: 16 (over z).
Axes of the slice: x: 8, y: 2, z: 16, core: 2. Of those that a mesh axis runs over, the one named last changes fastest.
The devices are a block of a 8x8x16 slice.
Arguments:
- series: float32 [800, 65536], P(None, ('subj', 'row', 'col')), parts along dimension 1, as said below
- keep_mask: int32 [512, 256], P(('subj', 'row'), 'col'), parts along dimension 0, may hold values from 0 to 1, as said below
- row_owner: int32 [512], P('subj'), parts along dimension 0, may hold values from 0 to 15, as said below
Outputs:
- owned_tiles: bfloat16 [32, 16, 96, 128, 128], P(('subj', 'row'), 'col'), parts along dimension 0
- owned_ids: int32 [32, 16, 96], P(('subj', 'row'), 'col'), parts along dimension 0
There are 2 independent parts, one for each index of `subj`. A program takes and returns all parts, laid end to end along the dimension named above; each array names one. Nothing has to cross between parts.
Inputs may be any that keep to these rules, and one draw needn't show every extreme that they name: Each voxel's series varies over time. `keep_mask`: of the 16 tiles that one tile row has in one column block, at most 6 are kept; in every draw one owner keeps exactly 6 in each of its tile rows in some column block. `row_owner`: the 16 tile rows of a row block have 16 different owners, and every owner holds 16 tile rows, from 16 different row blocks.
All inputs are finite; a program needn't handle non-finite values.
Results may differ from a plain program's by a relative error of at most 0.0042.
Values may be sent and summed in bfloat16 or wider, within the bound.
No kernel may reach another device: no remote copies, remote signals or barrier semaphores. Data moves between devices by JAX's collectives and lax.ppermute only.
A program may use at most 64 MiB of HBM per device.

v0:
```python
import jax
import jax.numpy as jnp
from jax import lax
from jax.sharding import PartitionSpec as P

TILE = 128
epsilon = 1e-05


def compact(flat_tiles, flat_ids, capacity):
    is_valid = (flat_ids >= 0).astype(jnp.int32)
    running = jnp.cumsum(is_valid)
    slot_index = jnp.arange(capacity, dtype=jnp.int32)
    position = jnp.arange(flat_ids.shape[0], dtype=jnp.int32)
    slot_hit = (is_valid[None, :] == 1) & (running[None, :] == slot_index[:, None] + 1)
    picked = jnp.sum(jnp.where(slot_hit, position[None, :], 0), axis=1)
    present = running[-1] > slot_index
    chosen = jnp.take(flat_tiles, picked, axis=0)
    slot_tiles = jnp.where(present[:, None, None], chosen, jnp.zeros_like(chosen))
    slot_ids = jnp.where(present, jnp.take(flat_ids, picked), -1).astype(jnp.int32)
    return (slot_tiles, slot_ids)


def shards(series, keep_mask, row_owner):
    frames = series.shape[0]
    average = jnp.mean(series, axis=0, keepdims=True)
    centred = series - average
    spread = jnp.mean(centred * centred, axis=0, keepdims=True)
    scored = (centred * lax.rsqrt(spread + epsilon)).astype(jnp.bfloat16)
    row_block = lax.all_gather(scored, "col", axis=1, tiled=True)
    product = lax.dot_general(
        row_block,
        lax.all_gather(scored, "row", axis=1, tiled=True),
        (((0,), (0,)), ((), ())),
        preferred_element_type=jnp.float32,
    )
    tile_grid = (product * (1.0 / frames)).astype(jnp.bfloat16)
    row_count, col_count = keep_mask.shape
    tile_grid = tile_grid.reshape(row_count, TILE, col_count, TILE).transpose(0, 2, 1, 3)
    row_devices = lax.axis_size("row")
    col_devices = lax.axis_size("col")
    row_index = lax.axis_index("row")
    col_index = lax.axis_index("col")
    total_cols = col_count * col_devices
    slot_limit = max(2, 3 * col_count // 8)
    capacity = row_count * slot_limit
    local_owner = lax.dynamic_slice_in_dim(row_owner, row_index * row_count, row_count)
    targets = jnp.arange(row_devices, dtype=jnp.int32)
    owns_row = local_owner[None, :] == targets[:, None]
    has_row = jnp.any(owns_row, axis=1)
    row_of = jnp.sum(
        jnp.where(owns_row, jnp.arange(row_count, dtype=jnp.int32)[None, :], 0), axis=1
    )
    keep_flags = jnp.where(has_row[:, None], jnp.take(keep_mask, row_of, axis=0), 0)
    global_row = row_index * row_count + row_of
    first_col = col_index * col_count
    running = jnp.cumsum(keep_flags, axis=1)
    slot_index = jnp.arange(slot_limit, dtype=jnp.int32)
    slot_hit = (keep_flags[:, None, :] == 1) & (
        running[:, None, :] == slot_index[None, :, None] + 1
    )
    picked = jnp.sum(
        jnp.where(slot_hit, jnp.arange(col_count, dtype=jnp.int32)[None, None, :], 0), axis=2
    )
    present = running[:, -1:] > slot_index[None, :]
    chosen = tile_grid[row_of[:, None], picked]
    outgoing = jnp.where(present[:, :, None, None], chosen, jnp.zeros_like(chosen))
    out_ids = jnp.where(present, global_row[:, None] * total_cols + first_col + picked, -1)
    incoming, in_ids = (
        lax.all_to_all(outgoing, "row", split_axis=0, concat_axis=0, tiled=True),
        lax.all_to_all(out_ids, "row", split_axis=0, concat_axis=0, tiled=True),
    )
    flat_tiles = incoming.reshape(-1, TILE, TILE)
    flat_ids = in_ids.reshape(-1)
    slot_tiles, slot_ids = compact(flat_tiles, flat_ids, capacity)
    return (slot_tiles.reshape(1, 1, capacity, TILE, TILE), slot_ids.reshape(1, 1, capacity))


def solution(mesh):
    in_specs = (P(None, ("subj", "row", "col")), P(("subj", "row"), "col"), P("subj"))
    out_specs = (P(("subj", "row"), "col", None, None, None), P(("subj", "row"), "col", None))
    return jax.shard_map(shards, mesh=mesh, in_specs=in_specs, out_specs=out_specs, check_vma=False)
```

profile of v0, /device:TPU:65, one launch (start us, length us, event | category | flops | bytes accessed | tf_op | source)
XLA Modules:
  0.0 313.3 jit_solution(12894685114126903149)
XLA Ops:
  7.3 1.1 reduce_sum.60
  8.4 1.1 multiply_reduce_fusion
  9.5 1.7 multiply_convert_fusion.1
  11.4 0.7 all-gather.5.cloned.1.call-update
  12.1 0.8 dynamic_slice.3
  13.0 0.6 gather_fusion
  14.4 0.7 copy.18
  15.1 44.6 %all-to-all-start = ((s32[16,1,6]{2,1,0:T(1,128)}), s32[16,1,6]{2,1,0:T(1,128)S(1)}, u32[]{:S(2)}, u32[]{:S(2)}) async-start(s32[16,1,6]{2,1,0:T(1,128)} %copy.18), calls=%async_computation | async-start | bytes 16384 | tf_op jit(solution)/shard_map/all_to_all | solution.py:71
  60.0 64.0 %all-gather.3.cloned.1.call-done = bf16[800,2048]{1,0:T(8,128)(2,1)} async-done(((bf16[800,128]{1,0:T(8,128)(2,1)}), bf16[800,2048]{1,0:T(8,128)(2,1)}) %all-gather.3.cloned.1.call-update) | async-done | bytes 3276816 | tf_op jit(solution)/shard_map/all_gather | solution.py:30
  124.0 61.5 %all-gather.5.cloned.1.call-done = bf16[800,2048]{1,0:T(8,128)(2,1)} async-done(((bf16[800,128]{1,0:T(8,128)(2,1)}), bf16[800,2048]{1,0:T(8,128)(2,1)}) %all-gather.5.cloned.1.call-update) | async-done | bytes 3276816 | tf_op jit(solution)/shard_map/all_gather | solution.py:33
  185.5 13.6 %fusion = bf16[256,8,16,128]{3,1,2,0:T(8,128)(2,1)} fusion(bf16[800,2048]{1,0:T(8,128)(2,1)} %all-gather.3.cloned.1.call-done, bf16[800,2048]{1,0:T(8,128)(2,1)} %all-gather.5.cloned.1.call-done), kind=kOutput, calls=%fused_computation.6 | convolution fusion | flops 6719275008 | bytes 14942208 | tf_op jit(solution)/shard_map/dot_general | solution.py:31
  199.2 9.7 %copy.22 = bf16[256,8,16,128]{3,2,1,0:T(8,128)(2,1)} copy(bf16[256,8,16,128]{3,1,2,0:T(8,128)(2,1)} %fusion) | data formatting | bytes 16777216
  208.9 9.1 %copy.24 = bf16[16,128,16,128]{3,1,2,0:T(8,128)(2,1)} copy(bf16[16,128,16,128]{3,2,1,0:T(8,128)(2,1)} %bitcast.36) | data formatting | bytes 16777216 | tf_op jit(solution)/shard_map/reshape | solution.py:39
  218.0 4.9 %gather_fusion.1 = bf16[96,128,128]{2,1,0:T(8,128)(2,1)S(1)} fusion(bf16[16,16,128,128]{3,2,1,0:T(8,128)(2,1)} %bitcast.37, s32[96]{0:T(128)S(1)} %reshape.311), kind=kCustom, calls=%fused_computation.1 | custom fusion | bytes 6292224 | tf_op jit(solution)/shard_map/gather | solution.py:66
  223.0 1.9 broadcast_select_fusion
  224.9 4.5 %all-to-all-start.1 = ((bf16[16,6,128,128]{3,2,1,0:T(8,128)(2,1)}), bf16[16,6,128,128]{3,2,1,0:T(8,128)(2,1)S(1)}, u32[]{:S(2)}, u32[]{:S(2)}) async-start(bf16[16,6,128,128]{3,2,1,0:T(8,128)(2,1)} %broadcast_select_fusion), calls=%async_computation.1 | async-start | bytes 6291456 | tf_op jit(solution)/shard_map/all_to_all | solution.py:70
  229.9 0.7 fusion.11
  230.9 0.6 slice.21
  231.8 1.2 gather_fusion.3
  233.1 0.7 compare_and_fusion
  233.8 1.2 compare_select_fusion.6
  235.0 65.3 %all-to-all-done.1 = bf16[16,6,128,128]{3,2,1,0:T(8,128)(2,1)S(1)} async-done(((bf16[16,6,128,128]{3,2,1,0:T(8,128)(2,1)}), bf16[16,6,128,128]{3,2,1,0:T(8,128)(2,1)S(1)}, u32[]{:S(2)}, u32[]{:S(2)}) %all-to-all-start.1) | async-done | bytes 3145760 | tf_op jit(solution)/shard_map/all_to_all | solution.py:70
  300.3 2.7 gather_fusion.2
  303.0 3.4 %fusion.1 = bf16[1,1,96,128,128]{4,3,2,1,0:T(8,128)(2,1)} fusion(bf16[96,128,128]{2,1,0:T(8,128)(2,1)} %gather_fusion.2, pred[96]{0:T(512)(128)(4,1)S(1)} %get-tuple-element.8, pred[96]{0:T(512)(128)(4,1)S(1)} %get-tuple-element.9), kind=kLoop, calls=%fused_computation.8 | loop fusion | flops 3145728 | bytes 6291648 | tf_op jit(solution)/shard_map/jit(_where)/select_n | solution.py:19
  (34 shorter events, 2.5 us)
Async XLA Ops:
  7.2 5.9 %copy-start = (s32[16,16]{1,0:T(8,128)S(1)}, s32[16,16]{1,0:T(8,128)}, u32[]{:S(2)}) copy-start(s32[16,16]{1,0:T(8,128)} %param.4) | copy-start | bytes 3076
  7.2 116.8 %all-gather.3.cloned.1.call-start = ((), (), s32[]{:S(2)}) async-start(), calls=%async_computation.2 | async-start | bytes 3481600 | tf_op jit(solution)/shard_map/all_gather | solution.py:30
  11.3 174.2 %all-gather.5.cloned.1.call-start = ((), (), s32[]{:S(2)}) async-start(), calls=%async_computation.3 | async-start | bytes 3481600 | tf_op jit(solution)/shard_map/all_gather | solution.py:33
  15.1 209.8 %all-to-all-start = ((s32[16,1,6]{2,1,0:T(1,128)}), s32[16,1,6]{2,1,0:T(1,128)S(1)}, u32[]{:S(2)}, u32[]{:S(2)}) async-start(s32[16,1,6]{2,1,0:T(1,128)} %copy.18), calls=%async_computation | async-start | bytes 16384 | tf_op jit(solution)/shard_map/all_to_all | solution.py:71
  224.9 75.4 %all-to-all-start.1 = ((bf16[16,6,128,128]{3,2,1,0:T(8,128)(2,1)}), bf16[16,6,128,128]{3,2,1,0:T(8,128)(2,1)S(1)}, u32[]{:S(2)}, u32[]{:S(2)}) async-start(bf16[16,6,128,128]{3,2,1,0:T(8,128)(2,1)} %broadcast_select_fusion), calls=%async_computation.1 | async-start | bytes 6291456 | tf_op jit(solution)/shard_map/all_to_all | solution.py:70
Sparse Core Ops, SparseCore 0:
  11.4 112.5 all-gather.2
  126.6 58.8 all-gather.4
where the time goes:
time: 314 us; the launch traced here: 313 us
  waiting for transfers between devices  192 us (61%)
  starting transfers between devices  49.2 us (16%)
  local copies, waits for them, and re-layouts  31.4 us (10%)
  between operations  14.2 us (5%)
  matrix products  13.6 us (4%)
  other arithmetic  13.2 us (4%)
    all_to_all x1, waiting for transfers between devices, shards(): lax.all_to_all(outgoing, 'row', split_axis=0, concat_axis=0, tiled=True)  65.3 us
    all_gather x1, waiting for transfers between devices, shards(): row_block = lax.all_gather(scored, 'col', axis=1, tiled=True)  64 us
    all_gather x1, waiting for transfers between devices, shards(): lax.all_gather(scored, 'row', axis=1, tiled=True)  61.5 us
    all_to_all x1, starting transfers between devices, shards(): lax.all_to_all(out_ids, 'row', split_axis=0, concat_axis=0, tiled=True)  44.6 us
    dot_general x1, matrix products, shards(): lax.dot_general(row_block, lax.all_gather(scored, 'row', axis=1, tiled=Tr...  13.6 us
    unnamed x3, local copies, waits for them, and re-layouts  9.76 us
    reshape x1, local copies, waits for them, and re-layouts, shards(): tile_grid.reshape(row_count, TILE, col_count, TILE).transpose(0, 2, 1, 3)  9.11 us
  transfers between devices with their start and end apart: 4, of which 3 were waited for; matrix products, arithmetic and copies ran while one was open for 15% of the time, Pallas kernels for 0%

commit v1 on v0

--- a/solution.py
+++ b/solution.py
@@ -27,7 +27,9 @@
     centred = series - average
     spread = jnp.mean(centred * centred, axis=0, keepdims=True)
     scored = (centred * lax.rsqrt(spread + epsilon)).astype(jnp.bfloat16)
-    row_block = lax.all_gather(scored, "col", axis=1, tiled=True)
+    row_block = jnp.concatenate(
+        lax.all_to_all(jnp.stack([scored] * lax.axis_size("col")), "col", 0, 0), axis=1
+    )
     product = lax.dot_general(
         row_block,
         lax.all_gather(scored, "row", axis=1, tiled=True),

time: 314 us -> 340 us (1.083)
  waiting for transfers between devices: 192 us -> 205 us
  starting transfers between devices: 49.2 us -> 61.8 us
    all_to_all x0 -> x1, waiting for transfers between devices: none -> 139 us  [shards(): lax.all_to_all(jnp.stack([scored] * lax.axis_size('col')), 'col', 0, 0)]
    all_gather x1 -> x0, waiting for transfers between devices: 64 us -> none  [shards(): row_block = lax.all_gather(scored, 'col', axis=1, tiled=True)]
    all_gather x1, waiting for transfers between devices: 61.5 us -> 0.02 us  [shards(): lax.all_gather(scored, 'row', axis=1, tiled=True)]
    all_to_all x0 -> x1, starting transfers between devices: none -> 44.4 us  [shards(): lax.all_to_all(jnp.stack([scored] * lax.axis_size('col')), 'col', 0, 0)]
    all_to_all x1, starting transfers between devices: 44.6 us -> 10.1 us  [shards(): lax.all_to_all(out_ids, 'row', split_axis=0, concat_axis=0, tiled=True)]
    unnamed x3 -> x7, local copies, waits for them, and re-layouts: 9.76 us -> 9.77 us
  transfers between devices with their start and end apart: 4 -> 4, of which waited for: 3 -> 2; matrix products, arithmetic and copies ran while one was open for 15% -> 14% of each run, Pallas kernels for 0% -> 0%
where the time goes in v1:
time: 340 us; the launch traced here: 339 us
  waiting for transfers between devices  205 us (60%)
  starting transfers between devices  61.8 us (18%)
  local copies, waits for them, and re-layouts  32.8 us (10%)
  between operations  14.2 us (4%)
  matrix products  13.1 us (4%)
  other arithmetic  12.6 us (4%)
    all_to_all x1, waiting for transfers between devices, shards(): lax.all_to_all(jnp.stack([scored] * lax.axis_size('col')), 'col', 0, 0)  139 us
    all_to_all x1, waiting for transfers between devices, shards(): lax.all_to_all(outgoing, 'row', split_axis=0, concat_axis=0, tiled=True)  65.3 us
    all_to_all x1, starting transfers between devices, shards(): lax.all_to_all(jnp.stack([scored] * lax.axis_size('col')), 'col', 0, 0)  44.4 us
    dot_general x1, matrix products, shards(): lax.dot_general(row_block, lax.all_gather(scored, 'row', axis=1, tiled=Tr...  13.1 us
    all_to_all x1, starting transfers between devices, shards(): lax.all_to_all(out_ids, 'row', split_axis=0, concat_axis=0, tiled=True)  10.1 us
    unnamed x7, local copies, waits for them, and re-layouts  9.77 us
    reshape x1, local copies, waits for them, and re-layouts, shards(): tile_grid.reshape(row_count, TILE, col_count, TILE).transpose(0, 2, 1, 3)  9.11 us
    all_to_all x1, starting transfers between devices, shards(): lax.all_to_all(outgoing, 'row', split_axis=0, concat_axis=0, tiled=True)  7.24 us
  transfers between devices with their start and end apart: 4, of which 2 were waited for; matrix products, arithmetic and copies ran while one was open for 14% of the time, Pallas kernels for 0%

profile of v1, /device:TPU:65, one launch (start us, length us, event | category | flops | bytes accessed | tf_op | source)
XLA Modules:
  0.0 339.5 jit_solution(17543250560020015228)
XLA Ops:
  7.2 1.1 reduce_sum.60
  8.3 1.1 multiply_reduce_fusion
  9.5 1.1 multiply_convert_fusion.1
  10.5 2.1 stack.2
  12.6 44.4 %all-to-all-start.1 = ((bf16[16,800,128]{2,1,0:T(8,128)(2,1)}), bf16[16,800,128]{2,1,0:T(8,128)(2,1)S(1)}, u32[]{:S(2)}, u32[]{:S(2)}) async-start(bf16[16,800,128]{2,1,0:T(8,128)(2,1)} %stack.2), calls=%async_computation.1 | async-start | bytes 6553600 | tf_op jit(solution)/shard_map/all_to_all | solution.py:31
  57.1 0.7 all-gather.2.cloned.1.call-update
  58.0 0.6 gather_fusion
  59.6 0.7 copy.19
  60.4 138.9 %all-to-all-done.1 = bf16[16,800,128]{2,1,0:T(8,128)(2,1)S(1)} async-done(((bf16[16,800,128]{2,1,0:T(8,128)(2,1)}), bf16[16,800,128]{2,1,0:T(8,128)(2,1)S(1)}, u32[]{:S(2)}, u32[]{:S(2)}) %all-to-all-start.1) | async-done | bytes 3276832 | tf_op jit(solution)/shard_map/all_to_all | solution.py:31
  199.3 10.1 %all-to-all-start = ((s32[16,1,6]{2,1,0:T(1,128)}), s32[16,1,6]{2,1,0:T(1,128)S(1)}, u32[]{:S(2)}, u32[]{:S(2)}) async-start(s32[16,1,6]{2,1,0:T(1,128)} %copy.19), calls=%async_computation | async-start | bytes 16384 | tf_op jit(solution)/shard_map/all_to_all | solution.py:73
  209.5 13.1 %fusion = bf16[256,8,16,128]{3,1,2,0:T(8,128)(2,1)} fusion(bf16[800,2048]{1,0:T(8,128)(2,1)} %all-gather.2.cloned.1.call-done, bf16[16,800,128]{2,1,0:T(8,128)(2,1)S(1)} %all-to-all-done.1), kind=kOutput, calls=%fused_computation.6 | convolution fusion | flops 6719275008 | bytes 14942208 | tf_op jit(solution)/shard_map/dot_general | solution.py:33
  222.5 9.7 %copy.25 = bf16[256,8,16,128]{3,2,1,0:T(8,128)(2,1)} copy(bf16[256,8,16,128]{3,1,2,0:T(8,128)(2,1)} %fusion) | data formatting | bytes 16777216
  232.3 9.1 %copy.31 = bf16[16,128,16,128]{3,1,2,0:T(8,128)(2,1)} copy(bf16[16,128,16,128]{3,2,1,0:T(8,128)(2,1)} %bitcast.43) | data formatting | bytes 16777216 | tf_op jit(solution)/shard_map/reshape | solution.py:41
  241.4 4.9 %gather_fusion.1 = bf16[96,128,128]{2,1,0:T(8,128)(2,1)S(1)} fusion(bf16[16,16,128,128]{3,2,1,0:T(8,128)(2,1)} %bitcast.44, s32[96]{0:T(128)S(1)} %reshape.321), kind=kCustom, calls=%fused_computation.1 | custom fusion | bytes 6292224 | tf_op jit(solution)/shard_map/gather | solution.py:68
  246.3 1.9 broadcast_select_fusion
  248.3 7.2 %all-to-all-start.2 = ((bf16[16,6,128,128]{3,2,1,0:T(8,128)(2,1)}), bf16[16,6,128,128]{3,2,1,0:T(8,128)(2,1)S(1)}, u32[]{:S(2)}, u32[]{:S(2)}) async-start(bf16[16,6,128,128]{3,2,1,0:T(8,128)(2,1)} %broadcast_select_fusion), calls=%async_computation.2 | async-start | bytes 6291456 | tf_op jit(solution)/shard_map/all_to_all | solution.py:72
  256.0 0.7 fusion.13
  257.1 0.6 slice.21
  258.0 1.2 gather_fusion.3
  259.2 0.7 compare_and_fusion
  259.9 1.2 compare_select_fusion.6
  261.1 65.3 %all-to-all-done.2 = bf16[16,6,128,128]{3,2,1,0:T(8,128)(2,1)S(1)} async-done(((bf16[16,6,128,128]{3,2,1,0:T(8,128)(2,1)}), bf16[16,6,128,128]{3,2,1,0:T(8,128)(2,1)S(1)}, u32[]{:S(2)}, u32[]{:S(2)}) %all-to-all-start.2) | async-done | bytes 3145760 | tf_op jit(solution)/shard_map/all_to_all | solution.py:72
  326.5 2.7 gather_fusion.2
  329.2 3.4 %fusion.3 = bf16[1,1,96,128,128]{4,3,2,1,0:T(8,128)(2,1)} fusion(bf16[96,128,128]{2,1,0:T(8,128)(2,1)} %gather_fusion.2, pred[96]{0:T(512)(128)(4,1)S(1)} %get-tuple-element.8, pred[96]{0:T(512)(128)(4,1)S(1)} %get-tuple-element.9), kind=kLoop, calls=%fused_computation.10 | loop fusion | flops 3145728 | bytes 6291648 | tf_op jit(solution)/shard_map/jit(_where)/select_n | solution.py:19
  (38 shorter events, 2.5 us)
Async XLA Ops:
  7.2 50.9 %copy-start = (s32[16,16]{1,0:T(8,128)S(1)}, s32[16,16]{1,0:T(8,128)}, u32[]{:S(2)}) copy-start(s32[16,16]{1,0:T(8,128)} %param.4) | copy-start | bytes 3076
  10.5 2.1 copy-start.1
  12.6 45.2 %copy-start.2 = (s32[256]{0:T(256)S(1)}, s32[256]{0:T(256)}, u32[]{:S(2)}) copy-start(s32[256]{0:T(256)} %param.5) | copy-start | bytes 3076
  12.6 186.7 %all-to-all-start.1 = ((bf16[16,800,128]{2,1,0:T(8,128)(2,1)}), bf16[16,800,128]{2,1,0:T(8,128)(2,1)S(1)}, u32[]{:S(2)}, u32[]{:S(2)}) async-start(bf16[16,800,128]{2,1,0:T(8,128)(2,1)} %stack.2), calls=%async_computation.1 | async-start | bytes 6553600 | tf_op jit(solution)/shard_map/all_to_all | solution.py:31
  57.0 152.5 %all-gather.2.cloned.1.call-start = ((), (), s32[]{:S(2)}) async-start(), calls=%async_computation.3 | async-start | bytes 3481600 | tf_op jit(solution)/shard_map/all_gather | solution.py:35
  199.3 49.0 %all-to-all-start = ((s32[16,1,6]{2,1,0:T(1,128)}), s32[16,1,6]{2,1,0:T(1,128)S(1)}, u32[]{:S(2)}, u32[]{:S(2)}) async-start(s32[16,1,6]{2,1,0:T(1,128)} %copy.19), calls=%async_computation | async-start | bytes 16384 | tf_op jit(solution)/shard_map/all_to_all | solution.py:73
  248.3 78.2 %all-to-all-start.2 = ((bf16[16,6,128,128]{3,2,1,0:T(8,128)(2,1)}), bf16[16,6,128,128]{3,2,1,0:T(8,128)(2,1)S(1)}, u32[]{:S(2)}, u32[]{:S(2)}) async-start(bf16[16,6,128,128]{3,2,1,0:T(8,128)(2,1)} %broadcast_select_fusion), calls=%async_computation.2 | async-start | bytes 6291456 | tf_op jit(solution)/shard_map/all_to_all | solution.py:72
Sparse Core Ops, SparseCore 0:
  60.5 54.4 all-gather.1
